TPU v7x, 8 devices: a whole 2x2x1 slice. The times are simulated.
8 devices in a mesh: data: 2 (over z, y), stage: 4 (over x, core).
Axes of the slice: x: 2, y: 2, z: 1, core: 2. Of those that a mesh axis runs over, the one named last changes fastest.
Arguments:
- master_up: float32 [4, 768, 3072], P('stage')
- master_down: float32 [4, 3072, 768], P('stage')
- mom1_up: float32 [4, 768, 3072], P('stage')
- mom1_down: float32 [4, 3072, 768], P('stage')
- mom2_up: float32 [4, 768, 3072], P('stage')
- mom2_down: float32 [4, 3072, 768], P('stage')
- grad_up: float32 [2, 4, 768, 3072], P('data', 'stage')
- grad_down: float32 [2, 4, 3072, 768], P('data', 'stage')
- stage_acts: bfloat16 [4, 8192, 768], P('stage', 'data')
- loss_grad: bfloat16 [8192, 768], P('data')
- next_batch: bfloat16 [2, 8192, 768], P(None, 'data')
- learn_rate: float32 [], replicated
- max_norm: float32 [], replicated
Outputs:
- output 1: float32 [4, 768, 3072], P('stage')
- output 2: float32 [4, 3072, 768], P('stage')
- output 3: float32 [4, 768, 3072], P('stage')
- output 4: float32 [4, 3072, 768], P('stage')
- output 5: float32 [4, 768, 3072], P('stage')
- output 6: float32 [4, 3072, 768], P('stage')
- output 7: bfloat16 [4, 2, 8192, 768], P('stage', None, 'data')
All inputs are finite; a program needn't handle non-finite values.
Results may differ from a plain program's by a relative error of at most 0.00896169.
Values are sent between devices in bfloat16 or wider.
A program may use at most 1 GiB of HBM per device.

v0:
```python
import functools

import jax
import jax.numpy as jnp
from jax import lax
from jax.experimental import pallas as pl
from jax.experimental.pallas import tpu as pltpu
from jax.sharding import PartitionSpec as P


BETA1 = 0.9
BETA2 = 0.95
ADAM_EPS = 1e-8
WEIGHT_DECAY = 0.1
NORM_EPS = 1e-6
ADAM_STEP = 8
SQRT_TWO_PI = 0.7978845608028654
GELU_CUBIC = 0.044715

BACK_ROWS = 256
FWD_ROWS = 256
HEAD = 128
BACK_TILE = 512
FWD_TILE = 512
PIECES = 6
F32_FIRST = ((0, 0),)
GROUPS = ((0, 0, 1), (1, 0, 2), (0, 1, 2), (1, 2, 2), (0, 3, 2), (1, 4, 2), (0, 5, 1))
TAIL = ((0, 1, 5), (1, 0, 6), (0, 5, 6))
STAGING = 3
WGRAD_STEP = 4096
SLAB = 16

BF16 = jnp.bfloat16
F32 = jnp.float32
MESH_ID = pl.DeviceIdType.MESH
ANY = pl.BlockSpec(memory_space=pl.ANY)
VMEM_LIMIT = 60 * 1024 * 1024
FWD_VMEM = 54000000
STORE_VMEM = 4 * 1024 * 1024
UPDATE_VMEM = 60 * 1024 * 1024


def dot_nn(left, right):
    return lax.dot_general(left, right, (((1,), (0,)), ((), ())), preferred_element_type=F32)


def dot_nt(left, right):
    return lax.dot_general(left, right, (((1,), (1,)), ((), ())), preferred_element_type=F32)


def dot_tn(left, right):
    return lax.dot_general(left, right, (((0,), (0,)), ((), ())), preferred_element_type=F32)


def span(index, size):
    if isinstance(index, int):
        return pl.ds(index * size, size)
    return pl.ds(pl.multiple_of(index * size, size), size)


def chunk_rows(c, total, size):
    if isinstance(c, int):
        return pl.ds(0 if c == 0 else total - HEAD, HEAD)
    return pl.ds(pl.multiple_of(HEAD + (c - 1) * size, HEAD), size)


def tanh_part(x, sq):
    return jnp.tanh(x * (SQRT_TWO_PI + (SQRT_TWO_PI * GELU_CUBIC) * sq))


def gelu_value(x):
    return x * (0.5 + 0.5 * tanh_part(x, x * x))


def gelu_pair(x):
    sq = x * x
    th = tanh_part(x, sq)
    half = 0.5 + 0.5 * th
    value = x * half
    slope = half + value * (1.0 - th) * (SQRT_TWO_PI + (3.0 * SQRT_TWO_PI * GELU_CUBIC) * sq)
    return value, slope


def meet_neighbours(stage, n_stages):
    barrier = pltpu.get_barrier_semaphore()

    @pl.when(stage > 0)
    def _():
        pl.semaphore_signal(barrier, inc=1, device_id={"stage": stage - 1}, device_id_type=MESH_ID)

    @pl.when(stage < n_stages - 1)
    def _():
        pl.semaphore_signal(barrier, inc=1, device_id={"stage": stage + 1}, device_id_type=MESH_ID)

    pl.semaphore_wait(barrier, jnp.minimum(stage, 1) + jnp.minimum(n_stages - 1 - stage, 1))


def back_kernel(n_stages, acts_ref, dy_ref, up32_ref, down32_ref, hid_ref, dpre_ref, gown_ref,
                up_ref, down_ref, a_buf, g_buf, h_buf, p_buf, dx_buf, acc_ref, pre_buf, dh_buf, stage_u, stage_v,
                u_sem, v_sem, a_sem, recv_sem, send_sem, gown_sem, h_sem, p_sem):
    stage = lax.axis_index("stage")
    last = n_stages - 1
    rows_all = g_buf.shape[0]
    hidden = up_ref.shape[1]
    n_chunks = rows_all // BACK_ROWS
    n_tiles = hidden // BACK_TILE

    def tile_copies(j):
        slot, cols = j % STAGING, pl.ds(j * BACK_TILE, BACK_TILE)
        return (pltpu.make_async_copy(up32_ref.at[0, :, cols], stage_u.at[slot], u_sem.at[slot]),
                pltpu.make_async_copy(down32_ref.at[0, cols, :], stage_v.at[slot], v_sem.at[slot]))

    def rows_of(c):
        return pl.ds(c * BACK_ROWS, BACK_ROWS) if isinstance(c, int) else span(c, BACK_ROWS)

    def a_copy(c):
        return pltpu.make_async_copy(acts_ref.at[0, rows_of(c), :], a_buf.at[rows_of(c), :], a_sem.at[c])

    def dy_copy(c):
        return pltpu.make_async_copy(dy_ref.at[rows_of(c), :], g_buf.at[rows_of(c), :], recv_sem.at[c])

    a_copy(0).start()

    @pl.when(stage == last)
    def _():
        dy_copy(0).start()

    for j in range(STAGING):
        for copy in tile_copies(j):
            copy.start()

    def load_rest(c, carry):
        a_copy(c).start()

        @pl.when(stage == last)
        def _():
            dy_copy(c).start()

        return carry

    def cast_tile(j):
        cols = pl.ds(j * BACK_TILE, BACK_TILE)
        for copy in tile_copies(j):
            copy.wait()
        up_ref[:, cols] = stage_u[j % STAGING].astype(BF16)
        down_ref[cols, :] = stage_v[j % STAGING].astype(BF16)
        if j + STAGING < n_tiles:
            for copy in tile_copies(j + STAGING):
                copy.start()
        if j == n_tiles - STAGING:
            lax.fori_loop(1, n_chunks, load_rest, 0)

    meet_neighbours(stage, n_stages)

    def send_of(c):
        return pltpu.make_async_remote_copy(
            src_ref=dx_buf.at[rows_of(c), :], dst_ref=g_buf.at[rows_of(c), :],
            send_sem=send_sem.at[c], recv_sem=recv_sem.at[c],
            device_id={"stage": stage - 1}, device_id_type=MESH_ID)

    def out_copies(c, slot):
        return (pltpu.make_async_copy(h_buf.at[slot], hid_ref.at[rows_of(c), :], h_sem.at[slot]),
                pltpu.make_async_copy(p_buf.at[slot], dpre_ref.at[rows_of(c), :], p_sem.at[slot]))

    def gown_copy(c):
        return pltpu.make_async_copy(g_buf.at[rows_of(c), :], gown_ref.at[rows_of(c), :], gown_sem.at[c])

    def chunk(c, carry, casting=False):
        slot = c % 2 if casting else lax.rem(c, 2)
        rows = rows_of(c)
        if not casting:
            @pl.when(c >= 2)
            def _():
                for copy in out_copies(c - 2, slot):
                    copy.wait()

        a_copy(c).wait()
        dy_copy(c).wait()
        gown_copy(c).start()

        def products(j):
            if casting:
                cast_tile(j)
            cols = pl.ds(j * BACK_TILE, BACK_TILE)
            pre_buf[j % 2] = dot_nn(a_buf[rows, :], up_ref[:, cols])
            dh_buf[j % 2] = dot_nt(g_buf[rows, :], down_ref[cols, :])

        def rest(j):
            cols = pl.ds(j * BACK_TILE, BACK_TILE)
            value, slope = gelu_pair(pre_buf[j % 2])
            h_buf[slot, :, cols] = value.astype(BF16)
            d_pre = (dh_buf[j % 2] * slope).astype(BF16)
            p_buf[slot, :, cols] = d_pre
            part = dot_nt(d_pre, up_ref[:, cols])
            if j == 0:
                acc_ref[...] = g_buf[rows, :].astype(F32) + part
            elif j < n_tiles - 1:
                acc_ref[...] += part
            else:
                dx_buf[rows, :] = (acc_ref[...] + part).astype(BF16)

        products(0)
        for j in range(n_tiles):
            if j + 1 < n_tiles:
                products(j + 1)
            rest(j)
        for copy in out_copies(c, slot):
            copy.start()

        @pl.when(stage > 0)
        def _():
            send_of(c).start()

        return carry

    @pl.when(stage == last)
    def _():
        chunk(0, 0, casting=True)

    @pl.when(stage < last)
    def _():
        for j in range(n_tiles):
            cast_tile(j)

    lax.fori_loop(stage // last, n_chunks, chunk, 0)

    for c in (n_chunks - 2, n_chunks - 1):
        for copy in out_copies(c, c % 2):
            copy.wait()

    def finish(c, carry):
        gown_copy(c).wait()

        @pl.when(stage > 0)
        def _():
            send_of(c).wait_send()

        return carry

    lax.fori_loop(0, n_chunks, finish, 0)


def backward(n_stages, acts, loss_grad, up32, down32):
    _, rows, width = acts.shape
    hidden = up32.shape[2]
    n_chunks = rows // BACK_ROWS
    wide = jax.ShapeDtypeStruct((rows, hidden), BF16)
    return pl.pallas_call(
        functools.partial(back_kernel, n_stages),
        name="backward",
        out_shape=(wide, wide, jax.ShapeDtypeStruct((rows, width), BF16)),
        in_specs=[ANY] * 4,
        out_specs=(ANY, ANY, ANY),
        scratch_shapes=[
            pltpu.VMEM((width, hidden), BF16),
            pltpu.VMEM((hidden, width), BF16),
            pltpu.VMEM((rows, width), BF16),
            pltpu.VMEM((rows, width), BF16),
            pltpu.VMEM((2, BACK_ROWS, hidden), BF16),
            pltpu.VMEM((2, BACK_ROWS, hidden), BF16),
            pltpu.VMEM((rows, width), BF16),
            pltpu.VMEM((BACK_ROWS, width), F32),
            pltpu.VMEM((2, BACK_ROWS, BACK_TILE), F32),
            pltpu.VMEM((2, BACK_ROWS, BACK_TILE), F32),
            pltpu.VMEM((STAGING, width, BACK_TILE), F32),
            pltpu.VMEM((STAGING, BACK_TILE, width), F32),
            pltpu.SemaphoreType.DMA((STAGING,)),
            pltpu.SemaphoreType.DMA((STAGING,)),
            pltpu.SemaphoreType.DMA((n_chunks,)),
            pltpu.SemaphoreType.DMA((n_chunks,)),
            pltpu.SemaphoreType.DMA((n_chunks,)),
            pltpu.SemaphoreType.DMA((n_chunks,)),
            pltpu.SemaphoreType.DMA((2,)),
            pltpu.SemaphoreType.DMA((2,)),
        ],
        compiler_params=pltpu.CompilerParams(collective_id=0, has_side_effects=True, vmem_limit_bytes=VMEM_LIMIT),
        cost_estimate=pl.CostEstimate(flops=6 * rows * width * hidden, bytes_accessed=6 * rows * hidden, transcendentals=rows * hidden),
    )(acts, loss_grad, up32, down32)


def wgrad_kernel(owner_ref, left_ref, right_ref, grad_ref, *refs):
    sum_refs, acc_ref = refs[:-1], refs[-1]
    lead = (0,) * (len(left_ref.shape) - 2)
    acc_ref[...] = grad_ref[0, 0]

    def step(k, carry):
        part = span(k, WGRAD_STEP)
        acc_ref[...] += dot_tn(left_ref[lead + (part, slice(None))], right_ref[part, :])
        return carry

    lax.fori_loop(0, right_ref.shape[0] // WGRAD_STEP, step, 0)
    for p, sum_ref in enumerate(sum_refs):
        def put(ref=sum_ref):
            ref[...] = acc_ref[...]

        if len(sum_refs) == 1:
            put()
        else:
            pl.when(pl.program_id(0) == p)(put)


def wgrad_units(kind, first, count, owner, left, right, grad):
    rows = right.shape[0]
    if kind == 0:
        half, piece = left.shape[2] // 2, right.shape[1] // PIECES
        shape = (half, piece)
        in_specs = [
            pl.BlockSpec((1, rows, half), lambda i, own: (0, 0, own[0])),
            pl.BlockSpec((rows, piece), lambda i, own: (0, first + i)),
            pl.BlockSpec((1, 1, half, piece), lambda i, own: (0, 0, own[0], first + i)),
        ]
    else:
        width, piece = right.shape[1], left.shape[1] // 2 // PIECES
        shape = (piece, width)
        in_specs = [
            pl.BlockSpec((rows, piece), lambda i, own: (0, own[0] * PIECES + first + i)),
            pl.BlockSpec((rows, width), lambda i, own: (0, 0)),
            pl.BlockSpec((1, 1, piece, width), lambda i, own: (0, 0, own[0] * PIECES + first + i, 0)),
        ]
    return pl.pallas_call(
        wgrad_kernel,
        out_shape=(jax.ShapeDtypeStruct(shape, F32),) * count,
        grid_spec=pltpu.PrefetchScalarGridSpec(
            num_scalar_prefetch=1,
            grid=(count,),
            in_specs=in_specs,
            out_specs=(pl.BlockSpec(shape, lambda i, own: (0, 0)),) * count,
            scratch_shapes=[pltpu.VMEM(shape, F32)],
        ),
        compiler_params=pltpu.CompilerParams(vmem_limit_bytes=VMEM_LIMIT),
        cost_estimate=pl.CostEstimate(flops=2 * rows * shape[0] * shape[1] * count, bytes_accessed=15 * 1024 * 1024, transcendentals=0),
    )(owner, left, right, grad)


def combine_kernel(scale, mine_ref, theirs_ref, sq_ref, gbar_ref, sq_out):
    n_rows, cols = mine_ref.shape

    def slab(i, fold):
        rows = span(i, SLAB)
        mean = (mine_ref[rows, :] + theirs_ref[rows, :]) * scale
        gbar_ref[rows, :] = mean
        part = jnp.sum((mean * mean).reshape(SLAB // 8, 8, cols), axis=0)
        for j in range(cols // 128):
            fold = fold + part[:, j * 128:(j + 1) * 128]
        return fold

    fold = lax.fori_loop(0, n_rows // SLAB, slab, jnp.zeros((8, 128), F32))
    first = pl.program_id(0) == 0

    @pl.when(first)
    def _():
        sq_out[...] = sq_ref[...] + fold

    @pl.when(jnp.logical_not(first))
    def _():
        sq_out[...] += fold


def combine(scale, mine, theirs, squares):
    rows, cols = mine.shape
    steps = 2
    spec = pl.BlockSpec((rows // steps, cols), lambda i: (i, 0))
    small = pl.BlockSpec((8, 128), lambda i: (0, 0))
    return pl.pallas_call(
        functools.partial(combine_kernel, scale),
        name="combine",
        out_shape=(jax.ShapeDtypeStruct((rows, cols), F32), jax.ShapeDtypeStruct((8, 128), F32)),
        grid=(steps,),
        in_specs=[spec, spec, small],
        out_specs=(spec, small),
        compiler_params=pltpu.CompilerParams(vmem_limit_bytes=VMEM_LIMIT),
        cost_estimate=pl.CostEstimate(flops=4 * rows * cols, bytes_accessed=12 * rows * cols, transcendentals=0),
    )(mine, theirs, squares)


def update_kernel(n_pieces, n_alias, want_bf16, owner_ref, lr_ref, clip_ref, w_ref, m_ref, v_ref, *rest):
    g_refs = rest[:n_pieces]
    w_out, m_out, v_out, last_out = rest[n_pieces + n_alias:]
    clip, lr = clip_ref[0:1, 0:1], lr_ref[0]

    def run(g_ref, b_out):
        def slab(i, carry):
            rows = span(i, SLAB)
            w = w_ref[0, rows, :]
            q = clip * g_ref[rows, :]
            m_new = BETA1 * m_ref[0, rows, :] + (1.0 - BETA1) * q
            v_new = BETA2 * v_ref[0, rows, :] + (1.0 - BETA2) * q * q
            m_hat = m_new * (1.0 / (1.0 - BETA1 ** ADAM_STEP))
            v_hat = v_new * (1.0 / (1.0 - BETA2 ** ADAM_STEP))
            w_new = w - lr * (m_hat / (jnp.sqrt(v_hat) + ADAM_EPS) + WEIGHT_DECAY * w)
            w_out[0, rows, :], m_out[0, rows, :], v_out[0, rows, :] = w_new, m_new, v_new
            if b_out is not None:
                b_out[rows, :] = w_new.astype(BF16)
            return carry

        lax.fori_loop(0, g_ref.shape[0] // SLAB, slab, 0)

    if n_pieces == 1:
        run(g_refs[0], last_out if want_bf16 else None)
    else:
        for p in range(n_pieces):
            pl.when(pl.program_id(0) == p)(functools.partial(run, g_refs[p], None))
    if not want_bf16:
        last_out[...] = clip_ref[...]


def update_units(kind, first, owner, knobs, state, grads, chain, want_bf16):
    rows, cols = grads[0].shape
    n = len(grads)
    steps = 2 if n == 1 else 1
    block = rows // steps
    if kind == 0:
        spec = pl.BlockSpec((1, block, cols), lambda p, i, own: (0, own[0] * steps + i, first + p))
    else:
        spec = pl.BlockSpec((1, block, cols), lambda p, i, own: (0, (own[0] * PIECES + first + p) * steps + i, 0))

    def piece_spec(q):
        return pl.BlockSpec((block, cols), lambda p, i, own: (jnp.clip((p - q) * steps + i, 0, steps - 1), 0))

    full = jax.ShapeDtypeStruct(state[0].shape, F32)
    out_shape, out_specs = (full,) * 3, (spec,) * 3
    if want_bf16:
        out_shape += (jax.ShapeDtypeStruct((rows, cols), BF16),)
        out_specs += (piece_spec(0),)
    else:
        out_shape += (jax.ShapeDtypeStruct((8, 128), F32),)
        out_specs += (pl.BlockSpec((8, 128), lambda p, i, own: (0, 0)),)
    size = n * rows * cols
    return pl.pallas_call(
        functools.partial(update_kernel, n, len(chain), want_bf16),
        out_shape=out_shape,
        grid_spec=pltpu.PrefetchScalarGridSpec(
            num_scalar_prefetch=1,
            grid=(n, steps),
            in_specs=[pl.BlockSpec(memory_space=pltpu.SMEM), pl.BlockSpec(memory_space=pltpu.VMEM)] + [spec] * 3 + [piece_spec(q) for q in range(n)] + [ANY] * len(chain),
            out_specs=out_specs,
        ),
        input_output_aliases={6 + n + i: i for i in range(len(chain))},
        compiler_params=pltpu.CompilerParams(vmem_limit_bytes=UPDATE_VMEM),
        cost_estimate=pl.CostEstimate(flops=30 * size, bytes_accessed=28 * size, transcendentals=size),
    )(owner, *knobs, *state, *grads, *chain)


def norm_kernel(n_stages, n_rep, sq_ref, max_ref, clip_ref, slots, send_sem, recv_sem):
    n_dev = n_stages * n_rep
    me = lax.axis_index("data") * n_stages + lax.axis_index("stage")
    slots[me] = sq_ref[...]

    def place(d):
        q = lax.rem(me + d, n_dev)
        return {"data": q // n_stages, "stage": lax.rem(q, n_stages)}

    barrier = pltpu.get_barrier_semaphore()
    for d in range(1, n_dev):
        pl.semaphore_signal(barrier, inc=1, device_id=place(d), device_id_type=MESH_ID)
    pl.semaphore_wait(barrier, n_dev - 1)
    copies = []
    for d in range(1, n_dev):
        copies.append(pltpu.make_async_remote_copy(
            src_ref=sq_ref, dst_ref=slots.at[me], send_sem=send_sem.at[d - 1], recv_sem=recv_sem.at[d - 1],
            device_id=place(d), device_id_type=MESH_ID))
        copies[-1].start()
    for copy in copies:
        copy.wait()
    square = slots[0]
    for q in range(1, n_dev):
        square = square + slots[q]
    total = jnp.full(clip_ref.shape, jnp.sum(square), F32)
    clip_ref[...] = jnp.minimum(1.0, max_ref[0] / (jnp.sqrt(total) + NORM_EPS))


def clip_factor(n_stages, n_rep, squares, max_norm):
    n_dev = n_stages * n_rep
    return pl.pallas_call(
        functools.partial(norm_kernel, n_stages, n_rep),
        name="clip_factor",
        out_shape=jax.ShapeDtypeStruct((8, 128), F32),
        in_specs=[pl.BlockSpec(memory_space=pltpu.VMEM), pl.BlockSpec(memory_space=pltpu.SMEM)],
        out_specs=pl.BlockSpec(memory_space=pltpu.VMEM),
        scratch_shapes=[
            pltpu.VMEM((n_dev, 8, 128), F32),
            pltpu.SemaphoreType.DMA((n_dev - 1,)),
            pltpu.SemaphoreType.DMA((n_dev - 1,)),
        ],
        compiler_params=pltpu.CompilerParams(collective_id=2, has_side_effects=True),
        cost_estimate=pl.CostEstimate(flops=40000000, bytes_accessed=4096, transcendentals=0),
    )(squares, max_norm)


def fwd_kernel(n_stages, n_rep, batch_ref, *refs):
    n_w = 2 * PIECES * n_rep
    w_refs = refs[:n_w]
    out_ref, up_ref, down_ref, x_buf, acc_ref, pre_buf, w_sem, recv_sem, send_sem = refs[n_w:]
    stage = lax.axis_index("stage")
    me = lax.axis_index("data")
    last = n_stages - 1
    total = x_buf.shape[0]
    hidden = up_ref.shape[1]
    n_tiles = hidden // FWD_TILE
    n_chunks = (total - 2 * HEAD) // FWD_ROWS + 2
    final = n_chunks - 1

    def rows_of(c):
        return chunk_rows(c, total, FWD_ROWS)

    def batch_copy(c):
        return pltpu.make_async_copy(batch_ref.at[rows_of(c), :], x_buf.at[rows_of(c), :], recv_sem.at[c])

    @pl.when(stage == 0)
    def _():
        batch_copy(0).start()

    copies = []
    for side in range(n_rep):
        owner = me if side == 0 else 1 - me
        for k in range(PIECES):
            u_src = w_refs[(2 * side) * PIECES + k]
            v_src = w_refs[(2 * side + 1) * PIECES + k]
            half_w, piece_n = u_src.shape
            piece_m = v_src.shape[0]
            u_dst = up_ref.at[span(owner, half_w), pl.ds(k * piece_n, piece_n)]
            v_dst = down_ref.at[span(owner * PIECES + k, piece_m), :]
            copies.append(pltpu.make_async_copy(u_src, u_dst, w_sem.at[len(copies)]))
            copies.append(pltpu.make_async_copy(v_src, v_dst, w_sem.at[len(copies)]))
    for copy in copies:
        copy.start()

    meet_neighbours(stage, n_stages)
    for copy in copies:
        copy.wait()

    @pl.when(stage == 0)
    def _():
        def load(c, carry):
            batch_copy(c).start()
            return carry

        lax.fori_loop(1, final, load, 0)
        load(final, 0)

    def send_of(c):
        return pltpu.make_async_remote_copy(
            src_ref=out_ref.at[rows_of(c), :], dst_ref=x_buf.at[rows_of(c), :],
            send_sem=send_sem.at[c], recv_sem=recv_sem.at[c],
            device_id={"stage": stage + 1}, device_id_type=MESH_ID)

    def chunk(c, carry):
        rows = rows_of(c)
        size = pl.ds(0, HEAD if isinstance(c, int) else FWD_ROWS)
        batch_copy(c).wait()

        def products(j):
            pre_buf[j % 2, size, :] = dot_nn(x_buf[rows, :], up_ref[:, pl.ds(j * FWD_TILE, FWD_TILE)])

        def rest(j):
            hid = gelu_value(pre_buf[j % 2, size, :]).astype(BF16)
            part = dot_nn(hid, down_ref[pl.ds(j * FWD_TILE, FWD_TILE), :])
            if j == 0:
                acc_ref[size, :] = x_buf[rows, :].astype(F32) + part
            elif j < n_tiles - 1:
                acc_ref[size, :] += part
            else:
                out_ref[rows, :] = (acc_ref[size, :] + part).astype(BF16)

        products(0)
        for j in range(n_tiles):
            if j + 1 < n_tiles:
                products(j + 1)
            rest(j)

        @pl.when(stage < last)
        def _():
            send_of(c).start()

        return carry

    chunk(0, 0)
    lax.fori_loop(1, final, chunk, 0)
    chunk(final, 0)

    @pl.when(stage < last)
    def _():
        def finish(c, carry):
            send_of(c).wait_send()
            return carry

        finish(0, 0)
        lax.fori_loop(1, final, finish, 0)
        finish(final, 0)


def forward(n_stages, n_rep, next_batch, weights):
    n_micro, rows, width = next_batch.shape
    total = n_micro * rows
    hidden = PIECES * weights[0].shape[1]
    n_chunks = (total - 2 * HEAD) // FWD_ROWS + 2
    return pl.pallas_call(
        functools.partial(fwd_kernel, n_stages, n_rep),
        name="forward",
        out_shape=pltpu.VMEM((total, width), BF16),
        in_specs=[ANY] * (1 + len(weights)),
        out_specs=pl.BlockSpec(memory_space=pltpu.VMEM),
        scratch_shapes=[
            pltpu.VMEM((width, hidden), BF16),
            pltpu.VMEM((hidden, width), BF16),
            pltpu.VMEM((total, width), BF16),
            pltpu.VMEM((FWD_ROWS, width), F32),
            pltpu.VMEM((2, FWD_ROWS, FWD_TILE), F32),
            pltpu.SemaphoreType.DMA((len(weights),)),
            pltpu.SemaphoreType.DMA((n_chunks,)),
            pltpu.SemaphoreType.DMA((n_chunks,)),
        ],
        compiler_params=pltpu.CompilerParams(collective_id=1, has_side_effects=True, vmem_limit_bytes=FWD_VMEM),
        cost_estimate=pl.CostEstimate(flops=4 * n_micro * rows * width * hidden, bytes_accessed=6 * rows * hidden, transcendentals=n_micro * rows * hidden),
    )(next_batch.reshape(total, width), *weights)


def store_kernel(y_ref, out_ref, sem):
    half = y_ref.shape[0] // 2
    copies = [pltpu.make_async_copy(y_ref.at[span(i, half), :], out_ref.at[span(i, half), :], sem.at[i]) for i in range(2)]
    for copy in copies:
        copy.start()
    for copy in copies:
        copy.wait()


def store(y):
    return pl.pallas_call(
        store_kernel,
        name="store",
        out_shape=jax.ShapeDtypeStruct(y.shape, y.dtype),
        in_specs=[pl.BlockSpec(memory_space=pltpu.VMEM)],
        out_specs=ANY,
        scratch_shapes=[pltpu.SemaphoreType.DMA((2,))],
        compiler_params=pltpu.CompilerParams(vmem_limit_bytes=STORE_VMEM),
        cost_estimate=pl.CostEstimate(flops=4000000, bytes_accessed=2 * y.size, transcendentals=0),
    )(y)


def part_of(parts):
    return next(iter(parts.values()))


def solution(mesh):
    n_stages = mesh.shape["stage"]
    n_rep = mesh.shape["data"]
    swap = [(i, n_rep - 1 - i) for i in range(n_rep)]

    def exchange(x):
        return lax.ppermute(x, "data", swap)

    def local_step(master_up, master_down, mom1_up, mom1_down, mom2_up, mom2_down, grad_up, grad_down, stage_acts, loss_grad, next_batch, learn_rate, max_norm):
        me = lax.axis_index("data")
        mine = jnp.reshape(me, (1,)).astype(jnp.int32)
        other = 1 - mine
        hid, d_pre, g_own = backward(n_stages, stage_acts, loss_grad, master_up, master_down)

        units = [(kind, first + i) for kind, first, count in GROUPS for i in range(count)]

        def wgrad(group, owner):
            kind, first, count = group
            operands = (stage_acts, d_pre, grad_up) if kind == 0 else (hid, g_own, grad_down)
            parts = wgrad_units(kind, first, count, owner, *operands)
            return {(kind, first + i): parts[i] for i in range(count)}

        arrived, whose = {}, other
        for group in GROUPS:
            parts = wgrad(group, whose)
            for unit, part in parts.items():
                arrived[unit] = exchange(part)
            whose = lax.optimization_barrier((other, part_of(parts)))[0]
        gbar, squares = {}, jnp.zeros((8, 128), F32)
        own_part = {}
        for kind in (0, 1):
            own_part.update(wgrad((kind, 0, PIECES), mine))
        for unit in units:
            gbar[unit], squares = combine(1.0 / n_rep, own_part[unit], arrived[unit], squares)
        clip = clip_factor(n_stages, n_rep, squares, jnp.reshape(max_norm, (1,)))
        knobs = (jnp.reshape(learn_rate, (1,)), clip)
        gbar_other = {}
        for unit in F32_FIRST:
            half = gbar[unit].shape[0] // 2
            top = exchange(gbar[unit][:half])
            low = exchange(lax.optimization_barrier((gbar[unit][half:], clip))[0])
            gbar_other[unit] = jnp.concatenate([top, low], axis=0)
        state = ((master_up, mom1_up, mom2_up), (master_down, mom1_down, mom2_down))
        chain = [(), ()]

        def update(unit, owner, grad):
            res = update_units(unit[0], unit[1], owner, knobs, state[unit[0]], [grad], chain[unit[0]], True)
            chain[unit[0]] = res[:3]
            return res[3]

        def update_group(kind, first, stop, clip):
            grads = [gbar_other[kind, k] for k in range(first, stop)]
            res = update_units(kind, first, other, (knobs[0], clip), state[kind], grads, chain[kind], False)
            chain[kind] = res[:3]
            return res[3]

        late = [unit for unit in units if unit not in F32_FIRST]
        own_w, other_w = {}, {}
        for unit in late + list(F32_FIRST):
            own_w[unit] = update(unit, mine, gbar[unit])
            if unit in late:
                other_w[unit] = exchange(own_w[unit])
        for unit in late:
            ready = lax.optimization_barrier((gbar[unit], own_w[late[-1]]))[0]
            gbar_other[unit] = exchange(ready)
        for unit in F32_FIRST:
            other_w[unit] = update(unit, other, gbar_other[unit])
        weights = []
        for side in (own_w, other_w):
            for kind in (0, 1):
                weights += [side[kind, k] for k in range(PIECES)]
        stage_outs = store(forward(n_stages, n_rep, next_batch, weights)).reshape((1,) + next_batch.shape)
        for kind, first, stop in TAIL:
            clip = update_group(kind, first, stop, clip)
        (new_up, new_m1_up, new_m2_up), (new_down, new_m1_down, new_m2_down) = chain
        return (new_up, new_down, new_m1_up, new_m1_down, new_m2_up, new_m2_down, stage_outs)

    w_spec = P("stage", None, None)
    g_spec = P("data", "stage", None, None)
    in_specs = (w_spec,) * 6 + (g_spec, g_spec, P("stage", "data", None), P("data", None), P(None, "data", None), P(), P())
    out_specs = (w_spec,) * 6 + (P("stage", None, "data", None),)
    return jax.shard_map(local_step, mesh=mesh, in_specs=in_specs, out_specs=out_specs, check_vma=False)
```

profile of v0, /device:TPU:3, one launch (start us, length us, event | category | flops | bytes accessed | tf_op | source)
XLA Modules:
  0.0 752.2 jit_solution(2635118059229724798)
XLA Ops:
  0.6 74.4 %backward.1 = (bf16[4096,3072]{1,0:T(8,128)(2,1)}, bf16[4096,3072]{1,0:T(8,128)(2,1)}, bf16[4096,768]{1,0:T(8,128)(2,1)}) custom-call(bf16[1,4096,768]{2,1,0:T(8,128)(2,1)} %left_ref.9, bf16[4096,768]{1,0:T(8,128)(2,1)} %dy_ref.1, f32[1,768,3072]{2,1,0:T(8,128)} %w_ref.31, f32[1,3072,768]{2,1,0:T(8,128)} %w_ref.30), custom_call_target="tpu_custom_call" | custom-call | flops 57982058496 | bytes 75497472 | tf_op jit(solution)/shard_map/backward/pallas_call | solution.py:248
  81.1 8.7 %shard_map.182 = (f32[256,768]{1,0:T(8,128)}, f32[256,768]{1,0:T(8,128)}) custom-call(s32[1]{0:T(128)S(6)} %sub.3.owner_ref, bf16[4096,3072]{1,0:T(8,128)(2,1)} %get-tuple-element.140.left_ref, bf16[4096,768]{1,0:T(8,128)(2,1)} %get-tuple-element.141.right_ref, f32[1,1,3072,768]{3,2,1,0:T(8,128)} %grad_ref.17), custom_call_target="tpu_custom_call" | custom-call | flops 3221225472 | bytes 15728640 | tf_op jit(solution)/shard_map/pallas_call | solution.py:320
  89.7 8.3 %shard_map.183 = (f32[384,512]{1,0:T(8,128)}, f32[384,512]{1,0:T(8,128)}) custom-call(s32[1]{0:T(128)S(6)} %sub.3.owner_ref, bf16[1,4096,768]{2,1,0:T(8,128)(2,1)} %left_ref.9, bf16[4096,3072]{1,0:T(8,128)(2,1)} %get-tuple-element.137.right_ref, f32[1,1,768,3072]{3,2,1,0:T(8,128)} %grad_ref.16), custom_call_target="tpu_custom_call" | custom-call | flops 3221225472 | bytes 15728640 | tf_op jit(solution)/shard_map/pallas_call | solution.py:320
  98.1 8.6 %shard_map.184 = (f32[256,768]{1,0:T(8,128)}, f32[256,768]{1,0:T(8,128)}) custom-call(s32[1]{0:T(128)S(6)} %sub.3.owner_ref, bf16[4096,3072]{1,0:T(8,128)(2,1)} %get-tuple-element.140.left_ref, bf16[4096,768]{1,0:T(8,128)(2,1)} %get-tuple-element.141.right_ref, f32[1,1,3072,768]{3,2,1,0:T(8,128)} %grad_ref.17), custom_call_target="tpu_custom_call" | custom-call | flops 3221225472 | bytes 15728640 | tf_op jit(solution)/shard_map/pallas_call | solution.py:320
  111.5 8.4 %shard_map.185 = (f32[384,512]{1,0:T(8,128)}, f32[384,512]{1,0:T(8,128)}) custom-call(s32[1]{0:T(128)S(6)} %sub.3.owner_ref, bf16[1,4096,768]{2,1,0:T(8,128)(2,1)} %left_ref.9, bf16[4096,3072]{1,0:T(8,128)(2,1)} %get-tuple-element.137.right_ref, f32[1,1,768,3072]{3,2,1,0:T(8,128)} %grad_ref.16), custom_call_target="tpu_custom_call" | custom-call | flops 3221225472 | bytes 15728640 | tf_op jit(solution)/shard_map/pallas_call | solution.py:320
  119.9 8.7 %shard_map.186 = (f32[256,768]{1,0:T(8,128)}, f32[256,768]{1,0:T(8,128)}) custom-call(s32[1]{0:T(128)S(6)} %sub.3.owner_ref, bf16[4096,3072]{1,0:T(8,128)(2,1)} %get-tuple-element.140.left_ref, bf16[4096,768]{1,0:T(8,128)(2,1)} %get-tuple-element.141.right_ref, f32[1,1,3072,768]{3,2,1,0:T(8,128)} %grad_ref.17), custom_call_target="tpu_custom_call" | custom-call | flops 3221225472 | bytes 15728640 | tf_op jit(solution)/shard_map/pallas_call | solution.py:320
  136.7 18.1 %shard_map.180 = (f32[384,512]{1,0:T(8,128)}, f32[384,512]{1,0:T(8,128)}, f32[384,512]{1,0:T(8,128)}, f32[384,512]{1,0:T(8,128)}, f32[384,512]{1,0:T(8,128)}, /*index=5*/f32[384,512]{1,0:T(8,128)}) custom-call(s32[1]{0:T(128)} %bitcast.owner_ref, bf16[1,4096,768]{2,1,0:T(8,128)(2,1)} %left_ref.9, bf16[4096,3072]{1,0:T(8,128)(2,1)} %get-tuple-element.137.right_ref, ...), custom_call_target="tpu_custom_call" | custom-call | flops 9663676416 | bytes 15728640 | tf_op jit(solution)/shard_map/pallas_call | solution.py:320
  154.9 45.2 %collective-permute-done.7.theirs_ref = f32[384,512]{1,0:T(8,128)S(1)} collective-permute-done((f32[384,512]{1,0:T(8,128)}, f32[384,512]{1,0:T(8,128)S(1)}, u32[]{:S(2)}, u32[]{:S(2)}) %collective-permute-start.7) | collective-permute-done | bytes 786464 | tf_op jit(solution)/shard_map/ppermute | solution.py:650
  201.6 15.3 %collective-permute-done.9.theirs_ref = f32[256,768]{1,0:T(8,128)} collective-permute-done((f32[256,768]{1,0:T(8,128)}, f32[256,768]{1,0:T(8,128)}, u32[]{:S(2)}, u32[]{:S(2)}) %collective-permute-start.9) | collective-permute-done | bytes 786464 | tf_op jit(solution)/shard_map/ppermute | solution.py:650
  219.6 17.5 %shard_map.188 = (f32[256,768]{1,0:T(8,128)}, f32[256,768]{1,0:T(8,128)}, f32[256,768]{1,0:T(8,128)}, f32[256,768]{1,0:T(8,128)}, f32[256,768]{1,0:T(8,128)}, /*index=5*/f32[256,768]{1,0:T(8,128)}) custom-call(s32[1]{0:T(128)} %bitcast.owner_ref, bf16[4096,3072]{1,0:T(8,128)(2,1)} %get-tuple-element.140.left_ref, ...), custom_call_target="tpu_custom_call" | custom-call | flops 9663676416 | bytes 15728640 | tf_op jit(solution)/shard_map/pallas_call | solution.py:320
  256.2 45.1 %collective-permute-done.3.theirs_ref = f32[384,512]{1,0:T(8,128)} collective-permute-done((f32[384,512]{1,0:T(8,128)}, f32[384,512]{1,0:T(8,128)}, u32[]{:S(2)}, u32[]{:S(2)}) %collective-permute-start.3) | collective-permute-done | bytes 786464 | tf_op jit(solution)/shard_map/ppermute | solution.py:650
  312.2 33.1 %clip_factor.1.clip_ref = f32[8,128]{1,0:T(8,128)} custom-call(f32[8,128]{1,0:T(8,128)} %get-tuple-element.179.sq_ref, f32[1]{0:T(128)} %bitcast.21.max_ref), custom_call_target="tpu_custom_call" | custom-call | flops 40000000 | bytes 4096 | tf_op jit(solution)/shard_map/clip_factor/pallas_call | solution.py:474
  382.1 7.2 collective-permute-done.27.refs_15_
  415.9 7.2 collective-permute-done.31.refs_19_
  424.3 24.0 %collective-permute-done.32.refs_20_ = bf16[256,768]{1,0:T(8,128)(2,1)S(1)} collective-permute-done((bf16[256,768]{1,0:T(8,128)(2,1)}, bf16[256,768]{1,0:T(8,128)(2,1)S(1)}, u32[]{:S(2)}, u32[]{:S(2)}) %collective-permute-start.32) | collective-permute-done | bytes 393248 | tf_op jit(solution)/shard_map/ppermute | solution.py:650
  449.5 7.2 collective-permute-done.33.refs_21_
  457.9 7.2 collective-permute-done.34.refs_22_
  491.8 15.7 %collective-permute-done.14.rest_2_ = f32[384,512]{1,0:T(8,128)} collective-permute-done((f32[384,512]{1,0:T(8,128)S(1)}, f32[384,512]{1,0:T(8,128)}, u32[]{:S(2)}, u32[]{:S(2)}) %collective-permute-start.14) | collective-permute-done | bytes 786464 | tf_op jit(solution)/shard_map/ppermute | solution.py:650
  508.6 15.7 %collective-permute-done.15.rest_3_ = f32[384,512]{1,0:T(8,128)} collective-permute-done((f32[384,512]{1,0:T(8,128)S(1)}, f32[384,512]{1,0:T(8,128)}, u32[]{:S(2)}, u32[]{:S(2)}) %collective-permute-start.15) | collective-permute-done | bytes 786464 | tf_op jit(solution)/shard_map/ppermute | solution.py:650
  525.5 15.7 %collective-permute-done.18.rest_0_ = f32[256,768]{1,0:T(8,128)} collective-permute-done((f32[256,768]{1,0:T(8,128)}, f32[256,768]{1,0:T(8,128)}, u32[]{:S(2)}, u32[]{:S(2)}) %collective-permute-start.18) | collective-permute-done | bytes 786464 | tf_op jit(solution)/shard_map/ppermute | solution.py:650
  542.3 15.7 %collective-permute-done.19.rest_1_ = f32[256,768]{1,0:T(8,128)} collective-permute-done((f32[256,768]{1,0:T(8,128)S(1)}, f32[256,768]{1,0:T(8,128)}, u32[]{:S(2)}, u32[]{:S(2)}) %collective-permute-start.19) | collective-permute-done | bytes 786464 | tf_op jit(solution)/shard_map/ppermute | solution.py:650
  559.2 157.1 %forward.1.y_ref = bf16[8192,768]{1,0:T(8,128)(2,1)S(1)} custom-call(bf16[8192,768]{1,0:T(8,128)(2,1)} %bitcast.23, bf16[384,512]{1,0:T(8,128)(2,1)} %get-tuple-element.255.refs_0_, bf16[384,512]{1,0:T(8,128)(2,1)} %get-tuple-element.256.refs_1_, bf16[384,512]{1,0:T(8,128)(2,1)} %get-tuple-element.257.refs_2_, bf16[384,512]{1,0:T(8,128)(2,1)} %get-tuple-element.258.refs_3_, ...), custom_call_target="tpu_custom_call" | custom-call | flops 77309411328 | bytes 75497472 | tf_op jit(solution)/shard_map/forward/pallas_call | solution.py:597
  721.1 11.5 %shard_map.196 = (f32[1,768,3072]{2,1,0:T(8,128)}, f32[1,768,3072]{2,1,0:T(8,128)}, f32[1,768,3072]{2,1,0:T(8,128)}, f32[8,128]{1,0:T(8,128)}) custom-call(s32[1]{0:T(128)S(6)} %sub.3.owner_ref, f32[1]{0:T(128)} %bitcast.12.lr_ref, f32[8,128]{1,0:T(8,128)} %clip_factor.1.clip_ref, ...), custom_call_target="tpu_custom_call", output_to_operand_aliasing={{0}: (10, {}), {1}: (11, {}), {2}: (12, {})} | custom-call | flops 23592960 | bytes 22020096 | tf_op jit(solution)/shard_map/pallas_call | solution.py:429
  732.6 15.5 %shard_map.203 = (f32[1,3072,768]{2,1,0:T(8,128)}, f32[1,3072,768]{2,1,0:T(8,128)}, f32[1,3072,768]{2,1,0:T(8,128)}, f32[8,128]{1,0:T(8,128)}) custom-call(s32[1]{0:T(128)S(6)} %sub.3.owner_ref, f32[1]{0:T(128)} %bitcast.19.lr_ref, f32[8,128]{1,0:T(8,128)} %get-tuple-element.213.clip_ref, ...), custom_call_target="tpu_custom_call", output_to_operand_aliasing={{0}: (12, {}), {1}: (13, {}), {2}: (14, {})} | custom-call | flops 35389440 | bytes 33030144 | tf_op jit(solution)/shard_map/pallas_call | solution.py:429
  (136 shorter events, 158.7 us)
Async XLA Ops:
  108.2 93.2 %collective-permute-start.8 = (f32[384,512]{1,0:T(8,128)}, f32[384,512]{1,0:T(8,128)S(1)}, u32[]{:S(2)}, u32[]{:S(2)}) collective-permute-start(f32[384,512]{1,0:T(8,128)} %get-tuple-element.144), channel_id=1, source_target_pairs={{0,4},{4,0},{1,5},{5,1},{2,6},{6,2},{3,7},{7,3}} | collective-permute-start | bytes 2359304 | tf_op jit(solution)/shard_map/ppermute | solution.py:650
  109.4 108.7 %collective-permute-start.10 = (f32[256,768]{1,0:T(8,128)}, f32[256,768]{1,0:T(8,128)S(1)}, u32[]{:S(2)}, u32[]{:S(2)}) collective-permute-start(f32[256,768]{1,0:T(8,128)} %get-tuple-element.142), channel_id=1, source_target_pairs={{0,4},{4,0},{1,5},{5,1},{2,6},{6,2},{3,7},{7,3}} | collective-permute-start | bytes 2359304 | tf_op jit(solution)/shard_map/ppermute | solution.py:650
  109.6 108.7 %collective-permute-start.11 = (f32[384,512]{1,0:T(8,128)}, f32[384,512]{1,0:T(8,128)}, u32[]{:S(2)}, u32[]{:S(2)}) collective-permute-start(f32[384,512]{1,0:T(8,128)} %shard_map.181), channel_id=1, source_target_pairs={{0,4},{4,0},{1,5},{5,1},{2,6},{6,2},{3,7},{7,3}} | collective-permute-start | bytes 2359304 | tf_op jit(solution)/shard_map/ppermute | solution.py:650
  135.3 64.9 %collective-permute-start.7 = (f32[384,512]{1,0:T(8,128)}, f32[384,512]{1,0:T(8,128)S(1)}, u32[]{:S(2)}, u32[]{:S(2)}) collective-permute-start(f32[384,512]{1,0:T(8,128)} %get-tuple-element.162), channel_id=1, source_target_pairs={{0,4},{4,0},{1,5},{5,1},{2,6},{6,2},{3,7},{7,3}} | collective-permute-start | bytes 2359304 | tf_op jit(solution)/shard_map/ppermute | solution.py:650
  135.5 81.4 %collective-permute-start.9 = (f32[256,768]{1,0:T(8,128)}, f32[256,768]{1,0:T(8,128)}, u32[]{:S(2)}, u32[]{:S(2)}) collective-permute-start(f32[256,768]{1,0:T(8,128)} %get-tuple-element.165), channel_id=1, source_target_pairs={{0,4},{4,0},{1,5},{5,1},{2,6},{6,2},{3,7},{7,3}} | collective-permute-start | bytes 2359304 | tf_op jit(solution)/shard_map/ppermute | solution.py:650
  200.2 103.4 %collective-permute-start.2 = (f32[256,768]{1,0:T(8,128)}, f32[256,768]{1,0:T(8,128)S(1)}, u32[]{:S(2)}, u32[]{:S(2)}) collective-permute-start(f32[256,768]{1,0:T(8,128)} %get-tuple-element.150), channel_id=1, source_target_pairs={{0,4},{4,0},{1,5},{5,1},{2,6},{6,2},{3,7},{7,3}} | collective-permute-start | bytes 2359304 | tf_op jit(solution)/shard_map/ppermute | solution.py:650
  201.4 52.5 %collective-permute-start.4 = (f32[384,512]{1,0:T(8,128)}, f32[384,512]{1,0:T(8,128)}, u32[]{:S(2)}, u32[]{:S(2)}) collective-permute-start(f32[384,512]{1,0:T(8,128)} %get-tuple-element.148), channel_id=1, source_target_pairs={{0,4},{4,0},{1,5},{5,1},{2,6},{6,2},{3,7},{7,3}} | collective-permute-start | bytes 2359304 | tf_op jit(solution)/shard_map/ppermute | solution.py:650
  216.9 92.1 %collective-permute-start = (f32[384,512]{1,0:T(8,128)}, f32[384,512]{1,0:T(8,128)S(1)}, u32[]{:S(2)}, u32[]{:S(2)}) collective-permute-start(f32[384,512]{1,0:T(8,128)} %shard_map.187), channel_id=1, source_target_pairs={{0,4},{4,0},{1,5},{5,1},{2,6},{6,2},{3,7},{7,3}} | collective-permute-start | bytes 2359304 | tf_op jit(solution)/shard_map/ppermute | solution.py:650
  218.2 88.6 %collective-permute-start.1 = (f32[256,768]{1,0:T(8,128)}, f32[256,768]{1,0:T(8,128)}, u32[]{:S(2)}, u32[]{:S(2)}) collective-permute-start(f32[256,768]{1,0:T(8,128)} %get-tuple-element.153), channel_id=1, source_target_pairs={{0,4},{4,0},{1,5},{5,1},{2,6},{6,2},{3,7},{7,3}} | collective-permute-start | bytes 2359304 | tf_op jit(solution)/shard_map/ppermute | solution.py:650
  218.4 82.9 %collective-permute-start.3 = (f32[384,512]{1,0:T(8,128)}, f32[384,512]{1,0:T(8,128)}, u32[]{:S(2)}, u32[]{:S(2)}) collective-permute-start(f32[384,512]{1,0:T(8,128)} %get-tuple-element.156), channel_id=1, source_target_pairs={{0,4},{4,0},{1,5},{5,1},{2,6},{6,2},{3,7},{7,3}} | collective-permute-start | bytes 2359304 | tf_op jit(solution)/shard_map/ppermute | solution.py:650
  380.9 42.2 %collective-permute-start.31 = (bf16[256,768]{1,0:T(8,128)(2,1)}, bf16[256,768]{1,0:T(8,128)(2,1)}, u32[]{:S(2)}, u32[]{:S(2)}) collective-permute-start(bf16[256,768]{1,0:T(8,128)(2,1)} %get-tuple-element.261.refs_7_), channel_id=1, source_target_pairs={{0,4},{4,0},{1,5},{5,1},{2,6},{6,2},{3,7},{7,3}} | collective-permute-start | bytes 1179656 | tf_op jit(solution)/shard_map/ppermute | solution.py:650
  389.4 85.4 %collective-permute-start.12 = (f32[384,512]{1,0:T(8,128)}, f32[384,512]{1,0:T(8,128)S(1)}, u32[]{:S(2)}, u32[]{:S(2)}) collective-permute-start(f32[384,512]{1,0:T(8,128)} %get-tuple-element.198.rest_0_), channel_id=1, source_target_pairs={{0,4},{4,0},{1,5},{5,1},{2,6},{6,2},{3,7},{7,3}} | collective-permute-start | bytes 2359304 | tf_op jit(solution)/shard_map/ppermute | solution.py:650
  406.5 50.3 %collective-permute-start.33 = (bf16[256,768]{1,0:T(8,128)(2,1)}, bf16[256,768]{1,0:T(8,128)(2,1)S(1)}, u32[]{:S(2)}, u32[]{:S(2)}) collective-permute-start(bf16[256,768]{1,0:T(8,128)(2,1)} %get-tuple-element.263.refs_9_), channel_id=1, source_target_pairs={{0,4},{4,0},{1,5},{5,1},{2,6},{6,2},{3,7},{7,3}} | collective-permute-start | bytes 1179656 | tf_op jit(solution)/shard_map/ppermute | solution.py:650
  414.7 50.5 %collective-permute-start.34 = (bf16[256,768]{1,0:T(8,128)(2,1)}, bf16[256,768]{1,0:T(8,128)(2,1)S(1)}, u32[]{:S(2)}, u32[]{:S(2)}) collective-permute-start(bf16[256,768]{1,0:T(8,128)(2,1)} %get-tuple-element.264.refs_10_), channel_id=1, source_target_pairs={{0,4},{4,0},{1,5},{5,1},{2,6},{6,2},{3,7},{7,3}} | collective-permute-start | bytes 1179656 | tf_op jit(solution)/shard_map/ppermute | solution.py:650
  423.2 50.5 %collective-permute-start.35 = (bf16[256,768]{1,0:T(8,128)(2,1)}, bf16[256,768]{1,0:T(8,128)(2,1)S(1)}, u32[]{:S(2)}, u32[]{:S(2)}) collective-permute-start(bf16[256,768]{1,0:T(8,128)(2,1)} %get-tuple-element.265.refs_11_), channel_id=1, source_target_pairs={{0,4},{4,0},{1,5},{5,1},{2,6},{6,2},{3,7},{7,3}} | collective-permute-start | bytes 1179656 | tf_op jit(solution)/shard_map/ppermute | solution.py:650
  456.8 50.7 %collective-permute-start.14 = (f32[384,512]{1,0:T(8,128)S(1)}, f32[384,512]{1,0:T(8,128)}, u32[]{:S(2)}, u32[]{:S(2)}) collective-permute-start(f32[384,512]{1,0:T(8,128)S(1)} %copy-done.3), channel_id=1, source_target_pairs={{0,4},{4,0},{1,5},{5,1},{2,6},{6,2},{3,7},{7,3}} | collective-permute-start | bytes 2359304 | tf_op jit(solution)/shard_map/ppermute | solution.py:650
  465.2 59.1 %collective-permute-start.15 = (f32[384,512]{1,0:T(8,128)S(1)}, f32[384,512]{1,0:T(8,128)}, u32[]{:S(2)}, u32[]{:S(2)}) collective-permute-start(f32[384,512]{1,0:T(8,128)S(1)} %copy-done.4), channel_id=1, source_target_pairs={{0,4},{4,0},{1,5},{5,1},{2,6},{6,2},{3,7},{7,3}} | collective-permute-start | bytes 2359304 | tf_op jit(solution)/shard_map/ppermute | solution.py:650
  473.6 67.5 %collective-permute-start.18 = (f32[256,768]{1,0:T(8,128)}, f32[256,768]{1,0:T(8,128)}, u32[]{:S(2)}, u32[]{:S(2)}) collective-permute-start(f32[256,768]{1,0:T(8,128)} %get-tuple-element.215.rest_0_), channel_id=1, source_target_pairs={{0,4},{4,0},{1,5},{5,1},{2,6},{6,2},{3,7},{7,3}} | collective-permute-start | bytes 2359304 | tf_op jit(solution)/shard_map/ppermute | solution.py:650
  474.8 83.2 %collective-permute-start.19 = (f32[256,768]{1,0:T(8,128)S(1)}, f32[256,768]{1,0:T(8,128)}, u32[]{:S(2)}, u32[]{:S(2)}) collective-permute-start(f32[256,768]{1,0:T(8,128)S(1)} %copy-done.1), channel_id=1, source_target_pairs={{0,4},{4,0},{1,5},{5,1},{2,6},{6,2},{3,7},{7,3}} | collective-permute-start | bytes 2359304 | tf_op jit(solution)/shard_map/ppermute | solution.py:650
  490.6 242.0 %collective-permute-start.20 = (f32[256,768]{1,0:T(8,128)}, f32[256,768]{1,0:T(8,128)}, u32[]{:S(2)}, u32[]{:S(2)}) collective-permute-start(f32[256,768]{1,0:T(8,128)} %get-tuple-element.219.rest_0_), channel_id=1, source_target_pairs={{0,4},{4,0},{1,5},{5,1},{2,6},{6,2},{3,7},{7,3}} | collective-permute-start | bytes 2359304 | tf_op jit(solution)/shard_map/ppermute | solution.py:650
  507.4 225.1 %collective-permute-start.21 = (f32[256,768]{1,0:T(8,128)}, f32[256,768]{1,0:T(8,128)}, u32[]{:S(2)}, u32[]{:S(2)}) collective-permute-start(f32[256,768]{1,0:T(8,128)} %get-tuple-element.221.rest_0_), channel_id=1, source_target_pairs={{0,4},{4,0},{1,5},{5,1},{2,6},{6,2},{3,7},{7,3}} | collective-permute-start | bytes 2359304 | tf_op jit(solution)/shard_map/ppermute | solution.py:650
  524.3 208.3 %collective-permute-start.22 = (f32[256,768]{1,0:T(8,128)}, f32[256,768]{1,0:T(8,128)}, u32[]{:S(2)}, u32[]{:S(2)}) collective-permute-start(f32[256,768]{1,0:T(8,128)} %get-tuple-element.223.rest_0_), channel_id=1, source_target_pairs={{0,4},{4,0},{1,5},{5,1},{2,6},{6,2},{3,7},{7,3}} | collective-permute-start | bytes 2359304 | tf_op jit(solution)/shard_map/ppermute | solution.py:650
  541.1 191.5 %collective-permute-start.23 = (f32[256,768]{1,0:T(8,128)}, f32[256,768]{1,0:T(8,128)}, u32[]{:S(2)}, u32[]{:S(2)}) collective-permute-start(f32[256,768]{1,0:T(8,128)} %get-tuple-element.225.rest_0_), channel_id=1, source_target_pairs={{0,4},{4,0},{1,5},{5,1},{2,6},{6,2},{3,7},{7,3}} | collective-permute-start | bytes 2359304 | tf_op jit(solution)/shard_map/ppermute | solution.py:650
  558.0 190.1 %collective-permute-start.24 = (f32[384,512]{1,0:T(8,128)}, f32[384,512]{1,0:T(8,128)}, u32[]{:S(2)}, u32[]{:S(2)}) collective-permute-start(f32[384,512]{1,0:T(8,128)} %get-tuple-element.245.rest_0_), channel_id=1, source_target_pairs={{0,4},{4,0},{1,5},{5,1},{2,6},{6,2},{3,7},{7,3}} | collective-permute-start | bytes 2359304 | tf_op jit(solution)/shard_map/ppermute | solution.py:650
  (34 other events, 943.7 us)
where the time goes:
time: 753 us; the launch traced here: 752 us
  Pallas kernels  471 us (63%)
  waiting for transfers between devices  242 us (32%)
  starting transfers between devices  32.8 us (4%)
    ppermute x36, waiting for transfers between devices, exchange(): return lax.ppermute(x, 'data', swap)  242 us
    pallas_call x1, Pallas kernels, forward(): pl.pallas_call(functools.partial(fwd_kernel, n_stages, n_rep), name='forw...  157 us
    pallas_call x9, Pallas kernels, wgrad_units(): pl.pallas_call(wgrad_kernel, out_shape=(jax.ShapeDtypeStruct(shape, F32),...  90.4 us
    pallas_call x16, Pallas kernels, update_units(): pl.pallas_call(functools.partial(update_kernel, n, len(chain), want_bf16)...  83.3 us
    pallas_call x1, Pallas kernels, backward(): pl.pallas_call(functools.partial(back_kernel, n_stages), name='backward',...  74.4 us
    pallas_call x1, Pallas kernels, clip_factor(): pl.pallas_call(functools.partial(norm_kernel, n_stages, n_rep), name='cli...  33.1 us
    ppermute x36, starting transfers between devices, exchange(): return lax.ppermute(x, 'data', swap)  32.8 us
    pallas_call x12, Pallas kernels, combine(): pl.pallas_call(functools.partial(combine_kernel, scale), name='combine',...  27.5 us
  transfers between devices with their start and end apart: 36, of which 16 were waited for; matrix products, arithmetic and copies ran while one was open for 0% of the time, Pallas kernels for 43%

commit v1 on v0

--- a/solution.py
+++ b/solution.py
@@ -27,8 +27,8 @@
 GROUPS = ((0, 0, 1), (1, 0, 2), (0, 1, 2), (1, 2, 2), (0, 3, 2), (1, 4, 2), (0, 5, 1))
 TAIL = ((0, 1, 5), (1, 0, 6), (0, 5, 6))
 STAGING = 3
-WGRAD_STEP = 4096
-SLAB = 16
+WGRAD_STEP = 2048
+SLAB = 32
 
 BF16 = jnp.bfloat16
 F32 = jnp.float32
@@ -506,10 +506,6 @@
     def batch_copy(c):
         return pltpu.make_async_copy(batch_ref.at[rows_of(c), :], x_buf.at[rows_of(c), :], recv_sem.at[c])
 
-    @pl.when(stage == 0)
-    def _():
-        batch_copy(0).start()
-
     copies = []
     for side in range(n_rep):
         owner = me if side == 0 else 1 - me
@@ -525,18 +521,19 @@
     for copy in copies:
         copy.start()
 
+    @pl.when(stage == 0)
+    def _():
+        def load(c, carry):
+            batch_copy(c).start()
+            return carry
+
+        load(0, 0)
+        lax.fori_loop(1, final, load, 0)
+        load(final, 0)
+
     meet_neighbours(stage, n_stages)
     for copy in copies:
         copy.wait()
-
-    @pl.when(stage == 0)
-    def _():
-        def load(c, carry):
-            batch_copy(c).start()
-            return carry
-
-        lax.fori_loop(1, final, load, 0)
-        load(final, 0)
 
     def send_of(c):
         return pltpu.make_async_remote_copy(

time: 753 us -> 754 us (level)
  transfers between devices with their start and end apart: 36 -> 36, of which waited for: 16 -> 17; matrix products, arithmetic and copies ran while one was open for 0% -> 0% of each run, Pallas kernels for 43% -> 43%
where the time goes in v1:
time: 754 us; the launch traced here: 753 us
  Pallas kernels  472 us (63%)
  waiting for transfers between devices  242 us (32%)
  starting transfers between devices  32.8 us (4%)
    ppermute x36, waiting for transfers between devices, exchange(): return lax.ppermute(x, 'data', swap)  242 us
    pallas_call x1, Pallas kernels, forward(): pl.pallas_call(functools.partial(fwd_kernel, n_stages, n_rep), name='forw...  157 us
    pallas_call x9, Pallas kernels, wgrad_units(): pl.pallas_call(wgrad_kernel, out_shape=(jax.ShapeDtypeStruct(shape, F32),...  96.2 us
    pallas_call x16, Pallas kernels, update_units(): pl.pallas_call(functools.partial(update_kernel, n, len(chain), want_bf16)...  79.2 us
    pallas_call x1, Pallas kernels, backward(): pl.pallas_call(functools.partial(back_kernel, n_stages), name='backward',...  74.4 us
    pallas_call x1, Pallas kernels, clip_factor(): pl.pallas_call(functools.partial(norm_kernel, n_stages, n_rep), name='cli...  33.1 us
    ppermute x36, starting transfers between devices, exchange(): return lax.ppermute(x, 'data', swap)  32.8 us
    pallas_call x12, Pallas kernels, combine(): pl.pallas_call(functools.partial(combine_kernel, scale), name='combine',...  27 us
  transfers between devices with their start and end apart: 36, of which 17 were waited for; matrix products, arithmetic and copies ran while one was open for 0% of the time, Pallas kernels for 43%

profile of v1, /device:TPU:3, one launch (start us, length us, event | category | flops | bytes accessed | tf_op | source)
XLA Modules:
  0.0 753.0 jit_solution(12375939647752102265)
XLA Ops:
  0.6 74.4 %backward.1 = (bf16[4096,3072]{1,0:T(8,128)(2,1)}, bf16[4096,3072]{1,0:T(8,128)(2,1)}, bf16[4096,768]{1,0:T(8,128)(2,1)}) custom-call(bf16[1,4096,768]{2,1,0:T(8,128)(2,1)} %left_ref.9, bf16[4096,768]{1,0:T(8,128)(2,1)} %dy_ref.1, f32[1,768,3072]{2,1,0:T(8,128)} %w_ref.31, f32[1,3072,768]{2,1,0:T(8,128)} %w_ref.30), custom_call_target="tpu_custom_call" | custom-call | flops 57982058496 | bytes 75497472 | tf_op jit(solution)/shard_map/backward/pallas_call | solution.py:248
  81.4 9.2 %shard_map.182 = (f32[256,768]{1,0:T(8,128)}, f32[256,768]{1,0:T(8,128)}) custom-call(s32[1]{0:T(128)S(6)} %sub.3.owner_ref, bf16[4096,3072]{1,0:T(8,128)(2,1)} %get-tuple-element.140.left_ref, bf16[4096,768]{1,0:T(8,128)(2,1)} %get-tuple-element.141.right_ref, f32[1,1,3072,768]{3,2,1,0:T(8,128)} %grad_ref.17), custom_call_target="tpu_custom_call" | custom-call | flops 3221225472 | bytes 15728640 | tf_op jit(solution)/shard_map/pallas_call | solution.py:320
  90.6 8.8 %shard_map.183 = (f32[384,512]{1,0:T(8,128)}, f32[384,512]{1,0:T(8,128)}) custom-call(s32[1]{0:T(128)S(6)} %sub.3.owner_ref, bf16[1,4096,768]{2,1,0:T(8,128)(2,1)} %left_ref.9, bf16[4096,3072]{1,0:T(8,128)(2,1)} %get-tuple-element.137.right_ref, f32[1,1,768,3072]{3,2,1,0:T(8,128)} %grad_ref.16), custom_call_target="tpu_custom_call" | custom-call | flops 3221225472 | bytes 15728640 | tf_op jit(solution)/shard_map/pallas_call | solution.py:320
  99.4 9.2 %shard_map.184 = (f32[256,768]{1,0:T(8,128)}, f32[256,768]{1,0:T(8,128)}) custom-call(s32[1]{0:T(128)S(6)} %sub.3.owner_ref, bf16[4096,3072]{1,0:T(8,128)(2,1)} %get-tuple-element.140.left_ref, bf16[4096,768]{1,0:T(8,128)(2,1)} %get-tuple-element.141.right_ref, f32[1,1,3072,768]{3,2,1,0:T(8,128)} %grad_ref.17), custom_call_target="tpu_custom_call" | custom-call | flops 3221225472 | bytes 15728640 | tf_op jit(solution)/shard_map/pallas_call | solution.py:320
  113.4 8.9 %shard_map.185 = (f32[384,512]{1,0:T(8,128)}, f32[384,512]{1,0:T(8,128)}) custom-call(s32[1]{0:T(128)S(6)} %sub.3.owner_ref, bf16[1,4096,768]{2,1,0:T(8,128)(2,1)} %left_ref.9, bf16[4096,3072]{1,0:T(8,128)(2,1)} %get-tuple-element.137.right_ref, f32[1,1,768,3072]{3,2,1,0:T(8,128)} %grad_ref.16), custom_call_target="tpu_custom_call" | custom-call | flops 3221225472 | bytes 15728640 | tf_op jit(solution)/shard_map/pallas_call | solution.py:320
  122.3 9.2 %shard_map.186 = (f32[256,768]{1,0:T(8,128)}, f32[256,768]{1,0:T(8,128)}) custom-call(s32[1]{0:T(128)S(6)} %sub.3.owner_ref, bf16[4096,3072]{1,0:T(8,128)(2,1)} %get-tuple-element.140.left_ref, bf16[4096,768]{1,0:T(8,128)(2,1)} %get-tuple-element.141.right_ref, f32[1,1,3072,768]{3,2,1,0:T(8,128)} %grad_ref.17), custom_call_target="tpu_custom_call" | custom-call | flops 3221225472 | bytes 15728640 | tf_op jit(solution)/shard_map/pallas_call | solution.py:320
  140.0 19.1 %shard_map.180 = (f32[384,512]{1,0:T(8,128)}, f32[384,512]{1,0:T(8,128)}, f32[384,512]{1,0:T(8,128)}, f32[384,512]{1,0:T(8,128)}, f32[384,512]{1,0:T(8,128)}, /*index=5*/f32[384,512]{1,0:T(8,128)}) custom-call(s32[1]{0:T(128)} %bitcast.owner_ref, bf16[1,4096,768]{2,1,0:T(8,128)(2,1)} %left_ref.9, bf16[4096,3072]{1,0:T(8,128)(2,1)} %get-tuple-element.137.right_ref, ...), custom_call_target="tpu_custom_call" | custom-call | flops 9663676416 | bytes 15728640 | tf_op jit(solution)/shard_map/pallas_call | solution.py:320
  159.0 43.0 %collective-permute-done.7.theirs_ref = f32[384,512]{1,0:T(8,128)S(1)} collective-permute-done((f32[384,512]{1,0:T(8,128)}, f32[384,512]{1,0:T(8,128)S(1)}, u32[]{:S(2)}, u32[]{:S(2)}) %collective-permute-start.7) | collective-permute-done | bytes 786464 | tf_op jit(solution)/shard_map/ppermute | solution.py:647
  203.5 15.3 %collective-permute-done.9.theirs_ref = f32[256,768]{1,0:T(8,128)} collective-permute-done((f32[256,768]{1,0:T(8,128)}, f32[256,768]{1,0:T(8,128)}, u32[]{:S(2)}, u32[]{:S(2)}) %collective-permute-start.9) | collective-permute-done | bytes 786464 | tf_op jit(solution)/shard_map/ppermute | solution.py:647
  221.5 19.1 %shard_map.188 = (f32[256,768]{1,0:T(8,128)}, f32[256,768]{1,0:T(8,128)}, f32[256,768]{1,0:T(8,128)}, f32[256,768]{1,0:T(8,128)}, f32[256,768]{1,0:T(8,128)}, /*index=5*/f32[256,768]{1,0:T(8,128)}) custom-call(s32[1]{0:T(128)} %bitcast.owner_ref, bf16[4096,3072]{1,0:T(8,128)(2,1)} %get-tuple-element.140.left_ref, ...), custom_call_target="tpu_custom_call" | custom-call | flops 9663676416 | bytes 15728640 | tf_op jit(solution)/shard_map/pallas_call | solution.py:320
  259.3 43.8 %collective-permute-done.3.theirs_ref = f32[384,512]{1,0:T(8,128)} collective-permute-done((f32[384,512]{1,0:T(8,128)}, f32[384,512]{1,0:T(8,128)}, u32[]{:S(2)}, u32[]{:S(2)}) %collective-permute-start.3) | collective-permute-done | bytes 786464 | tf_op jit(solution)/shard_map/ppermute | solution.py:647
  313.9 33.1 %clip_factor.1.clip_ref = f32[8,128]{1,0:T(8,128)} custom-call(f32[8,128]{1,0:T(8,128)} %get-tuple-element.179.sq_ref, f32[1]{0:T(128)} %bitcast.21.max_ref), custom_call_target="tpu_custom_call" | custom-call | flops 40000000 | bytes 4096 | tf_op jit(solution)/shard_map/clip_factor/pallas_call | solution.py:474
  383.8 7.2 collective-permute-done.27.refs_15_
  409.2 7.2 collective-permute-done.30.refs_18_
  417.6 7.2 collective-permute-done.31.refs_19_
  426.0 24.0 %collective-permute-done.32.refs_20_ = bf16[256,768]{1,0:T(8,128)(2,1)S(1)} collective-permute-done((bf16[256,768]{1,0:T(8,128)(2,1)}, bf16[256,768]{1,0:T(8,128)(2,1)S(1)}, u32[]{:S(2)}, u32[]{:S(2)}) %collective-permute-start.32) | collective-permute-done | bytes 393248 | tf_op jit(solution)/shard_map/ppermute | solution.py:647
  451.2 7.2 collective-permute-done.33.refs_21_
  493.4 15.7 %collective-permute-done.14.rest_2_ = f32[384,512]{1,0:T(8,128)} collective-permute-done((f32[384,512]{1,0:T(8,128)S(1)}, f32[384,512]{1,0:T(8,128)}, u32[]{:S(2)}, u32[]{:S(2)}) %collective-permute-start.14) | collective-permute-done | bytes 786464 | tf_op jit(solution)/shard_map/ppermute | solution.py:647
  510.3 15.7 %collective-permute-done.15.rest_3_ = f32[384,512]{1,0:T(8,128)} collective-permute-done((f32[384,512]{1,0:T(8,128)S(1)}, f32[384,512]{1,0:T(8,128)}, u32[]{:S(2)}, u32[]{:S(2)}) %collective-permute-start.15) | collective-permute-done | bytes 786464 | tf_op jit(solution)/shard_map/ppermute | solution.py:647
  527.1 15.7 %collective-permute-done.18.rest_0_ = f32[256,768]{1,0:T(8,128)} collective-permute-done((f32[256,768]{1,0:T(8,128)}, f32[256,768]{1,0:T(8,128)}, u32[]{:S(2)}, u32[]{:S(2)}) %collective-permute-start.18) | collective-permute-done | bytes 786464 | tf_op jit(solution)/shard_map/ppermute | solution.py:647
  544.0 15.7 %collective-permute-done.19.rest_1_ = f32[256,768]{1,0:T(8,128)} collective-permute-done((f32[256,768]{1,0:T(8,128)S(1)}, f32[256,768]{1,0:T(8,128)}, u32[]{:S(2)}, u32[]{:S(2)}) %collective-permute-start.19) | collective-permute-done | bytes 786464 | tf_op jit(solution)/shard_map/ppermute | solution.py:647
  560.9 156.9 %forward.1.y_ref = bf16[8192,768]{1,0:T(8,128)(2,1)S(1)} custom-call(bf16[8192,768]{1,0:T(8,128)(2,1)} %bitcast.23, bf16[384,512]{1,0:T(8,128)(2,1)} %get-tuple-element.255.refs_0_, bf16[384,512]{1,0:T(8,128)(2,1)} %get-tuple-element.256.refs_1_, bf16[384,512]{1,0:T(8,128)(2,1)} %get-tuple-element.257.refs_2_, bf16[384,512]{1,0:T(8,128)(2,1)} %get-tuple-element.258.refs_3_, ...), custom_call_target="tpu_custom_call" | custom-call | flops 77309411328 | bytes 75497472 | tf_op jit(solution)/shard_map/forward/pallas_call | solution.py:594
  722.6 10.9 %shard_map.196 = (f32[1,768,3072]{2,1,0:T(8,128)}, f32[1,768,3072]{2,1,0:T(8,128)}, f32[1,768,3072]{2,1,0:T(8,128)}, f32[8,128]{1,0:T(8,128)}) custom-call(s32[1]{0:T(128)S(6)} %sub.3.owner_ref, f32[1]{0:T(128)} %bitcast.12.lr_ref, f32[8,128]{1,0:T(8,128)} %clip_factor.1.clip_ref, ...), custom_call_target="tpu_custom_call", output_to_operand_aliasing={{0}: (10, {}), {1}: (11, {}), {2}: (12, {})} | custom-call | flops 23592960 | bytes 22020096 | tf_op jit(solution)/shard_map/pallas_call | solution.py:429
  733.5 15.7 %shard_map.203 = (f32[1,3072,768]{2,1,0:T(8,128)}, f32[1,3072,768]{2,1,0:T(8,128)}, f32[1,3072,768]{2,1,0:T(8,128)}, f32[8,128]{1,0:T(8,128)}) custom-call(s32[1]{0:T(128)S(6)} %sub.3.owner_ref, f32[1]{0:T(128)} %bitcast.19.lr_ref, f32[8,128]{1,0:T(8,128)} %get-tuple-element.213.clip_ref, ...), custom_call_target="tpu_custom_call", output_to_operand_aliasing={{0}: (12, {}), {1}: (13, {}), {2}: (14, {})} | custom-call | flops 35389440 | bytes 33030144 | tf_op jit(solution)/shard_map/pallas_call | solution.py:429
  (136 shorter events, 158.4 us)
Async XLA Ops:
  110.0 93.2 %collective-permute-start.8 = (f32[384,512]{1,0:T(8,128)}, f32[384,512]{1,0:T(8,128)S(1)}, u32[]{:S(2)}, u32[]{:S(2)}) collective-permute-start(f32[384,512]{1,0:T(8,128)} %get-tuple-element.144), channel_id=1, source_target_pairs={{0,4},{4,0},{1,5},{5,1},{2,6},{6,2},{3,7},{7,3}} | collective-permute-start | bytes 2359304 | tf_op jit(solution)/shard_map/ppermute | solution.py:647
  111.3 108.7 %collective-permute-start.10 = (f32[256,768]{1,0:T(8,128)}, f32[256,768]{1,0:T(8,128)S(1)}, u32[]{:S(2)}, u32[]{:S(2)}) collective-permute-start(f32[256,768]{1,0:T(8,128)} %get-tuple-element.142), channel_id=1, source_target_pairs={{0,4},{4,0},{1,5},{5,1},{2,6},{6,2},{3,7},{7,3}} | collective-permute-start | bytes 2359304 | tf_op jit(solution)/shard_map/ppermute | solution.py:647
  111.5 108.7 %collective-permute-start.11 = (f32[384,512]{1,0:T(8,128)}, f32[384,512]{1,0:T(8,128)}, u32[]{:S(2)}, u32[]{:S(2)}) collective-permute-start(f32[384,512]{1,0:T(8,128)} %shard_map.181), channel_id=1, source_target_pairs={{0,4},{4,0},{1,5},{5,1},{2,6},{6,2},{3,7},{7,3}} | collective-permute-start | bytes 2359304 | tf_op jit(solution)/shard_map/ppermute | solution.py:647
  138.5 63.5 %collective-permute-start.7 = (f32[384,512]{1,0:T(8,128)}, f32[384,512]{1,0:T(8,128)S(1)}, u32[]{:S(2)}, u32[]{:S(2)}) collective-permute-start(f32[384,512]{1,0:T(8,128)} %get-tuple-element.162), channel_id=1, source_target_pairs={{0,4},{4,0},{1,5},{5,1},{2,6},{6,2},{3,7},{7,3}} | collective-permute-start | bytes 2359304 | tf_op jit(solution)/shard_map/ppermute | solution.py:647
  138.7 80.0 %collective-permute-start.9 = (f32[256,768]{1,0:T(8,128)}, f32[256,768]{1,0:T(8,128)}, u32[]{:S(2)}, u32[]{:S(2)}) collective-permute-start(f32[256,768]{1,0:T(8,128)} %get-tuple-element.165), channel_id=1, source_target_pairs={{0,4},{4,0},{1,5},{5,1},{2,6},{6,2},{3,7},{7,3}} | collective-permute-start | bytes 2359304 | tf_op jit(solution)/shard_map/ppermute | solution.py:647
  202.0 103.4 %collective-permute-start.2 = (f32[256,768]{1,0:T(8,128)}, f32[256,768]{1,0:T(8,128)S(1)}, u32[]{:S(2)}, u32[]{:S(2)}) collective-permute-start(f32[256,768]{1,0:T(8,128)} %get-tuple-element.150), channel_id=1, source_target_pairs={{0,4},{4,0},{1,5},{5,1},{2,6},{6,2},{3,7},{7,3}} | collective-permute-start | bytes 2359304 | tf_op jit(solution)/shard_map/ppermute | solution.py:647
  203.3 53.8 %collective-permute-start.4 = (f32[384,512]{1,0:T(8,128)}, f32[384,512]{1,0:T(8,128)}, u32[]{:S(2)}, u32[]{:S(2)}) collective-permute-start(f32[384,512]{1,0:T(8,128)} %get-tuple-element.148), channel_id=1, source_target_pairs={{0,4},{4,0},{1,5},{5,1},{2,6},{6,2},{3,7},{7,3}} | collective-permute-start | bytes 2359304 | tf_op jit(solution)/shard_map/ppermute | solution.py:647
  218.8 92.0 %collective-permute-start = (f32[384,512]{1,0:T(8,128)}, f32[384,512]{1,0:T(8,128)S(1)}, u32[]{:S(2)}, u32[]{:S(2)}) collective-permute-start(f32[384,512]{1,0:T(8,128)} %shard_map.187), channel_id=1, source_target_pairs={{0,4},{4,0},{1,5},{5,1},{2,6},{6,2},{3,7},{7,3}} | collective-permute-start | bytes 2359304 | tf_op jit(solution)/shard_map/ppermute | solution.py:647
  220.0 88.5 %collective-permute-start.1 = (f32[256,768]{1,0:T(8,128)}, f32[256,768]{1,0:T(8,128)}, u32[]{:S(2)}, u32[]{:S(2)}) collective-permute-start(f32[256,768]{1,0:T(8,128)} %get-tuple-element.153), channel_id=1, source_target_pairs={{0,4},{4,0},{1,5},{5,1},{2,6},{6,2},{3,7},{7,3}} | collective-permute-start | bytes 2359304 | tf_op jit(solution)/shard_map/ppermute | solution.py:647
  220.2 82.9 %collective-permute-start.3 = (f32[384,512]{1,0:T(8,128)}, f32[384,512]{1,0:T(8,128)}, u32[]{:S(2)}, u32[]{:S(2)}) collective-permute-start(f32[384,512]{1,0:T(8,128)} %get-tuple-element.156), channel_id=1, source_target_pairs={{0,4},{4,0},{1,5},{5,1},{2,6},{6,2},{3,7},{7,3}} | collective-permute-start | bytes 2359304 | tf_op jit(solution)/shard_map/ppermute | solution.py:647
  391.0 85.4 %collective-permute-start.12 = (f32[384,512]{1,0:T(8,128)}, f32[384,512]{1,0:T(8,128)S(1)}, u32[]{:S(2)}, u32[]{:S(2)}) collective-permute-start(f32[384,512]{1,0:T(8,128)} %get-tuple-element.198.rest_0_), channel_id=1, source_target_pairs={{0,4},{4,0},{1,5},{5,1},{2,6},{6,2},{3,7},{7,3}} | collective-permute-start | bytes 2359304 | tf_op jit(solution)/shard_map/ppermute | solution.py:647
  407.3 42.7 %collective-permute-start.32 = (bf16[256,768]{1,0:T(8,128)(2,1)}, bf16[256,768]{1,0:T(8,128)(2,1)S(1)}, u32[]{:S(2)}, u32[]{:S(2)}) collective-permute-start(bf16[256,768]{1,0:T(8,128)(2,1)} %get-tuple-element.262.refs_8_), channel_id=1, source_target_pairs={{0,4},{4,0},{1,5},{5,1},{2,6},{6,2},{3,7},{7,3}} | collective-permute-start | bytes 1179656 | tf_op jit(solution)/shard_map/ppermute | solution.py:647
  408.0 50.5 %collective-permute-start.33 = (bf16[256,768]{1,0:T(8,128)(2,1)}, bf16[256,768]{1,0:T(8,128)(2,1)S(1)}, u32[]{:S(2)}, u32[]{:S(2)}) collective-permute-start(bf16[256,768]{1,0:T(8,128)(2,1)} %get-tuple-element.263.refs_9_), channel_id=1, source_target_pairs={{0,4},{4,0},{1,5},{5,1},{2,6},{6,2},{3,7},{7,3}} | collective-permute-start | bytes 1179656 | tf_op jit(solution)/shard_map/ppermute | solution.py:647
  416.4 50.5 %collective-permute-start.34 = (bf16[256,768]{1,0:T(8,128)(2,1)}, bf16[256,768]{1,0:T(8,128)(2,1)S(1)}, u32[]{:S(2)}, u32[]{:S(2)}) collective-permute-start(bf16[256,768]{1,0:T(8,128)(2,1)} %get-tuple-element.264.refs_10_), channel_id=1, source_target_pairs={{0,4},{4,0},{1,5},{5,1},{2,6},{6,2},{3,7},{7,3}} | collective-permute-start | bytes 1179656 | tf_op jit(solution)/shard_map/ppermute | solution.py:647
  424.9 50.5 %collective-permute-start.35 = (bf16[256,768]{1,0:T(8,128)(2,1)}, bf16[256,768]{1,0:T(8,128)(2,1)S(1)}, u32[]{:S(2)}, u32[]{:S(2)}) collective-permute-start(bf16[256,768]{1,0:T(8,128)(2,1)} %get-tuple-element.265.refs_11_), channel_id=1, source_target_pairs={{0,4},{4,0},{1,5},{5,1},{2,6},{6,2},{3,7},{7,3}} | collective-permute-start | bytes 1179656 | tf_op jit(solution)/shard_map/ppermute | solution.py:647
  458.5 50.7 %collective-permute-start.14 = (f32[384,512]{1,0:T(8,128)S(1)}, f32[384,512]{1,0:T(8,128)}, u32[]{:S(2)}, u32[]{:S(2)}) collective-permute-start(f32[384,512]{1,0:T(8,128)S(1)} %copy-done.3), channel_id=1, source_target_pairs={{0,4},{4,0},{1,5},{5,1},{2,6},{6,2},{3,7},{7,3}} | collective-permute-start | bytes 2359304 | tf_op jit(solution)/shard_map/ppermute | solution.py:647
  466.9 59.1 %collective-permute-start.15 = (f32[384,512]{1,0:T(8,128)S(1)}, f32[384,512]{1,0:T(8,128)}, u32[]{:S(2)}, u32[]{:S(2)}) collective-permute-start(f32[384,512]{1,0:T(8,128)S(1)} %copy-done.4), channel_id=1, source_target_pairs={{0,4},{4,0},{1,5},{5,1},{2,6},{6,2},{3,7},{7,3}} | collective-permute-start | bytes 2359304 | tf_op jit(solution)/shard_map/ppermute | solution.py:647
  475.3 67.5 %collective-permute-start.18 = (f32[256,768]{1,0:T(8,128)}, f32[256,768]{1,0:T(8,128)}, u32[]{:S(2)}, u32[]{:S(2)}) collective-permute-start(f32[256,768]{1,0:T(8,128)} %get-tuple-element.215.rest_0_), channel_id=1, source_target_pairs={{0,4},{4,0},{1,5},{5,1},{2,6},{6,2},{3,7},{7,3}} | collective-permute-start | bytes 2359304 | tf_op jit(solution)/shard_map/ppermute | solution.py:647
  476.5 83.2 %collective-permute-start.19 = (f32[256,768]{1,0:T(8,128)S(1)}, f32[256,768]{1,0:T(8,128)}, u32[]{:S(2)}, u32[]{:S(2)}) collective-permute-start(f32[256,768]{1,0:T(8,128)S(1)} %copy-done.1), channel_id=1, source_target_pairs={{0,4},{4,0},{1,5},{5,1},{2,6},{6,2},{3,7},{7,3}} | collective-permute-start | bytes 2359304 | tf_op jit(solution)/shard_map/ppermute | solution.py:647
  492.3 241.2 %collective-permute-start.20 = (f32[256,768]{1,0:T(8,128)}, f32[256,768]{1,0:T(8,128)}, u32[]{:S(2)}, u32[]{:S(2)}) collective-permute-start(f32[256,768]{1,0:T(8,128)} %get-tuple-element.219.rest_0_), channel_id=1, source_target_pairs={{0,4},{4,0},{1,5},{5,1},{2,6},{6,2},{3,7},{7,3}} | collective-permute-start | bytes 2359304 | tf_op jit(solution)/shard_map/ppermute | solution.py:647
  509.1 224.4 %collective-permute-start.21 = (f32[256,768]{1,0:T(8,128)}, f32[256,768]{1,0:T(8,128)}, u32[]{:S(2)}, u32[]{:S(2)}) collective-permute-start(f32[256,768]{1,0:T(8,128)} %get-tuple-element.221.rest_0_), channel_id=1, source_target_pairs={{0,4},{4,0},{1,5},{5,1},{2,6},{6,2},{3,7},{7,3}} | collective-permute-start | bytes 2359304 | tf_op jit(solution)/shard_map/ppermute | solution.py:647
  526.0 207.5 %collective-permute-start.22 = (f32[256,768]{1,0:T(8,128)}, f32[256,768]{1,0:T(8,128)}, u32[]{:S(2)}, u32[]{:S(2)}) collective-permute-start(f32[256,768]{1,0:T(8,128)} %get-tuple-element.223.rest_0_), channel_id=1, source_target_pairs={{0,4},{4,0},{1,5},{5,1},{2,6},{6,2},{3,7},{7,3}} | collective-permute-start | bytes 2359304 | tf_op jit(solution)/shard_map/ppermute | solution.py:647
  542.8 190.7 %collective-permute-start.23 = (f32[256,768]{1,0:T(8,128)}, f32[256,768]{1,0:T(8,128)}, u32[]{:S(2)}, u32[]{:S(2)}) collective-permute-start(f32[256,768]{1,0:T(8,128)} %get-tuple-element.225.rest_0_), channel_id=1, source_target_pairs={{0,4},{4,0},{1,5},{5,1},{2,6},{6,2},{3,7},{7,3}} | collective-permute-start | bytes 2359304 | tf_op jit(solution)/shard_map/ppermute | solution.py:647
  559.7 189.5 %collective-permute-start.24 = (f32[384,512]{1,0:T(8,128)}, f32[384,512]{1,0:T(8,128)}, u32[]{:S(2)}, u32[]{:S(2)}) collective-permute-start(f32[384,512]{1,0:T(8,128)} %get-tuple-element.245.rest_0_), channel_id=1, source_target_pairs={{0,4},{4,0},{1,5},{5,1},{2,6},{6,2},{3,7},{7,3}} | collective-permute-start | bytes 2359304 | tf_op jit(solution)/shard_map/ppermute | solution.py:647
  (34 other events, 959.5 us)
